TPU v7x, 32 devices: a whole 2x2x4 slice. The times are simulated.
32 devices in a mesh: row: 4 (over x, core), col: 8 (over z, y).
Axes of the slice: x: 2, y: 2, z: 4, core: 2. Of those that a mesh axis runs over, the one named last changes fastest.
Arguments:
- users: bfloat16 [32768, 256], P(('row', 'col')), may hold values from -20 to 20
- positives: int32 [32768], P(('row', 'col')), may hold values from 0 to 511
- items: bfloat16 [512, 256], P(('row', 'col')), may hold values from -6 to 6
- item_ids: int32 [512], P(('row', 'col')), may hold values from 0 to 999999
Outputs:
- loss: float32 [32768], P(('row', 'col'))
All inputs are finite; a program needn't handle non-finite values.
Results may differ from a plain program's by a relative error of at most 0.0003.
Values may be sent and summed in bfloat16 or wider, within the bound.
No kernel may reach another device: no remote copies, remote signals or barrier semaphores. Data moves between devices by JAX's collectives and lax.ppermute only.
A program may use at most 128 MiB of HBM per device.

v0:
```python
import jax
import jax.numpy as jnp
from jax import lax
from jax.sharding import PartitionSpec as P


def absorb(carry, users, positives, pos_id, table, piece, where_at):
    high, summed, chosen = carry
    scores = 0.125 * lax.dot_general(
        users, piece, (((1,), (1,)), ((), ())), preferred_element_type=jnp.float32
    )
    ids = jnp.take(table, where_at)
    hit = where_at[None, :] == positives[:, None]
    keep = (ids[None, :] != pos_id[:, None]) | hit
    masked = jnp.where(keep, scores, -1e30)
    new_high = jnp.maximum(high, jnp.max(masked, axis=1))
    terms = jnp.where(keep, jnp.exp(masked - new_high[:, None]), 0.0)
    summed = jnp.sum(terms, axis=1)
    chosen = jnp.sum(jnp.where(hit, scores, 0.0), axis=1)
    return (new_high, summed, chosen)


def per_device(users, positives, items, item_ids):
    table = lax.all_gather(item_ids, ("row", "col"), axis=0, tiled=True)
    pos_id = jnp.take(table, positives)
    user_rows = users.shape[0]
    init = (
        jnp.full((user_rows,), -1e30, jnp.float32),
        jnp.zeros((user_rows,), jnp.float32),
        jnp.zeros((user_rows,), jnp.float32),
    )
    piece = lax.all_gather(items, ("row", "col"), axis=0, tiled=True)
    where_at = jnp.arange(piece.shape[0], dtype=jnp.int32)
    carry = absorb(init, users, positives, pos_id, table, piece, where_at)
    high, summed, chosen = carry
    return high + jnp.log(summed) - chosen


def solution(mesh):
    in_specs = (
        P(("row", "col"), None),
        P(("row", "col")),
        P(("row", "col"), None),
        P(("row", "col")),
    )
    out_specs = P(("row", "col"))
    return jax.shard_map(
        per_device, mesh=mesh, in_specs=in_specs, out_specs=out_specs, check_vma=False
    )
```

profile of v0, /device:TPU:0, one launch (start us, length us, event | category | flops | bytes accessed | tf_op | source)
XLA Modules:
  0.0 123.0 jit_solution(11870605535669868126)
XLA Ops:
  0.0 0.0 copy-start
  0.0 0.0 copy-start.1
  0.0 0.9 dynamic-update-slice
  0.9 42.0 %all-reduce = s32[512]{0:T(512)S(1)} all-reduce(s32[512]{0:T(512)S(1)} %dynamic-update-slice), channel_id=1, replica_groups=mesh['row'=4,'col'=8] {'row','col'}, use_global_device_ids=true, to_apply=%add | all-reduce | flops 512 | bytes 4096
  42.9 3.5 %gather_fusion = s32[512]{0:T(512)S(1)} fusion(s32[512]{0:T(512)S(1)} %all-reduce, s32[1024]{0:T(1024)S(1)} %pad_clamp_fusion), kind=kCustom, calls=%fused_computation | custom fusion | bytes 6144 | tf_op jit(solution)/shard_map/jit(_take)/gather | solution.py:12
  46.4 0.0 copy-done.1
  46.4 0.0 copy-start.2
  46.4 6.9 %gather_fusion.1 = s32[1024]{0:T(1024)S(1)} fusion(s32[512]{0:T(512)S(1)} %all-reduce, s32[1024]{0:T(1024)S(1)} %fusion.2), kind=kCustom, calls=%fused_computation.1 | custom fusion | bytes 12288 | tf_op jit(solution)/shard_map/jit(_take)/gather | solution.py:25
  53.3 0.0 copy-done.2
  53.3 67.4 %all_gather.7 = bf16[512,256]{1,0:T(8,128)(2,1)S(1)} all-gather(bf16[16,256]{1,0:T(8,128)(2,1)S(1)} %copy-done.2), channel_id=1, replica_groups=mesh['row'=4,'col'=8] {'row','col'}, dimensions={0}, use_global_device_ids=true | all-gather | bytes 270336 | tf_op jit(solution)/shard_map/all_gather | solution.py:32
  120.7 0.0 copy-done
  120.7 0.6 fusion.1
  121.4 1.0 select_reduce_fusion.1
  122.4 0.6 add_subtract_fusion
  (7 shorter events, 0.0 us)
Async XLA Ops:
  0.0 120.7 %copy-start = (bf16[1024,256]{1,0:T(8,128)(2,1)S(1)}, bf16[1024,256]{1,0:T(8,128)(2,1)}, u32[]{:S(2)}) copy-start(bf16[1024,256]{1,0:T(8,128)(2,1)} %param.4) | copy-start | bytes 1572868
  0.0 46.4 %copy-start.1 = (s32[1024]{0:T(1024)S(1)}, s32[1024]{0:T(1024)}, u32[]{:S(2)}) copy-start(s32[1024]{0:T(1024)} %param.5) | copy-start | bytes 12292
  46.4 6.9 %copy-start.2 = (bf16[16,256]{1,0:T(8,128)(2,1)S(1)}, bf16[16,256]{1,0:T(8,128)(2,1)}, u32[]{:S(2)}) copy-start(bf16[16,256]{1,0:T(8,128)(2,1)} %param.6) | copy-start | bytes 24580
where the time goes:
time: 123 us
  blocking collectives  109 us (89%)
  local copies, waits for them, and re-layouts  11.3 us (9%)
  other arithmetic  1.67 us (1%)
    all_gather x1, blocking collectives, per_device(): piece = lax.all_gather(items, ('row', 'col'), axis=0, tiled=True)  67.4 us
    unnamed x1, blocking collectives  42 us
    gather x1, local copies, waits for them, and re-layouts, per_device(): pos_id = jnp.take(table, positives)  6.87 us
    gather x1, local copies, waits for them, and re-layouts, absorb(): ids = jnp.take(table, where_at)  3.49 us

commit v1 on v0

v1 whole, which is shorter than its diff:
```python
import functools
import math

import jax
import jax.numpy as jnp
from jax import lax
from jax.experimental import pallas as pl
from jax.experimental.pallas import tpu as pltpu
from jax.sharding import PartitionSpec as P

LANES = 128
SUB = 8
BASE = 256
DIGITS = 3
LOW = -1e30


def pack_kernel(items_ref, ids_ref, out_ref):
    rows, width = items_ref.shape
    groups = rows // SUB
    span = LANES // groups
    copies = out_ref.shape[0]
    row = lax.broadcasted_iota(jnp.int32, (SUB, LANES), 0)
    lane = lax.broadcasted_iota(jnp.int32, (SUB, LANES), 1)
    held = jnp.zeros((SUB, LANES), jnp.int32)
    for k in range(rows):
        group = k // SUB
        mine = (row == k % SUB) & (lane >= group * span) & (lane < (group + 1) * span)
        held = jnp.where(mine, ids_ref[k], held)
    place = lane % span
    digit = jnp.zeros((SUB, LANES), jnp.int32)
    for d in range(DIGITS):
        digit = jnp.where(place == d, (held // BASE**d) % BASE, digit)
    tail = digit.astype(jnp.float32).astype(jnp.bfloat16)
    cols = [items_ref[:, c * LANES : (c + 1) * LANES] for c in range(width // LANES)]
    for n in range(copies):
        for c, col in enumerate(cols):
            out_ref[n, c * rows : (c + 1) * rows, :] = col
        out_ref[n, len(cols) * rows :, :] = tail


def pack(items, ids, copies):
    rows, width = items.shape
    tall = rows * (width // LANES) + SUB
    return pl.pallas_call(
        pack_kernel,
        out_shape=jax.ShapeDtypeStruct((copies, tall, LANES), items.dtype),
        in_specs=[
            pl.BlockSpec(memory_space=pltpu.VMEM),
            pl.BlockSpec(memory_space=pltpu.SMEM),
        ],
        out_specs=pl.BlockSpec(memory_space=pltpu.VMEM),
        compiler_params=pltpu.CompilerParams(vmem_limit_bytes=(2 << 20) + 4 * copies * tall * LANES),
        name="pack",
    )(items, ids)


def repeat(count, body, init):
    return body(0, init) if count == 1 else lax.fori_loop(0, count, body, init)


def loss_kernel(rows, pool_ref, users_ref, pos_ref, out_ref, score_ref, id_ref):
    devices = pool_ref.shape[0]
    users, width = users_ref.shape
    cols = width // LANES
    groups = rows // SUB
    span = LANES // groups
    wide = score_ref.shape[1]
    batch = math.gcd(devices, max(1, 512 // rows))
    blocks = devices // batch
    tiles = batch * groups
    rate = 0.125 / math.log(2)

    k = lax.broadcasted_iota(jnp.int32, (LANES, groups * LANES), 0)
    g = lax.broadcasted_iota(jnp.int32, (LANES, groups * LANES), 1) // LANES
    weigh = jnp.zeros((LANES, groups * LANES), jnp.float32)
    for d in range(DIGITS):
        weigh = jnp.where(k == g * span + d, float(BASE**d), weigh)
    weigh = weigh.astype(jnp.bfloat16)

    def decode(b, _):
        digit = pool_ref[pl.ds(b * batch, batch), cols * rows :, :].reshape(batch * SUB, LANES)
        id_ref[pl.ds(b * batch * SUB, batch * SUB), :] = jnp.dot(
            digit, weigh, preferred_element_type=jnp.float32
        )
        return 0

    repeat(blocks, decode, 0)

    def ids(b, t):
        d, g = divmod(t, groups)
        return id_ref[pl.ds((b * batch + d) * SUB, SUB), g * LANES : (g + 1) * LANES]

    up = lax.broadcasted_iota(jnp.int32, (SUB, LANES), 0)
    zero = jnp.zeros((SUB, LANES), jnp.float32)

    for u in range(users // wide):

        def multiply(b, _):
            pool = jnp.concatenate(
                [
                    pool_ref[pl.ds(b * batch, batch), c * rows : (c + 1) * rows, :].reshape(batch * rows, LANES)
                    for c in range(cols)
                ],
                axis=1,
            )
            score_ref[pl.ds(b * batch * rows, batch * rows), :] = lax.dot_general(
                pool, users_ref[u * wide : (u + 1) * wide, :], (((1,), (1,)), ((), ())),
                preferred_element_type=jnp.float32,
            )
            return 0

        repeat(blocks, multiply, 0)
        for v in range(wide // LANES):
            at = u * wide + v * LANES

            def place(b, t):
                return pl.ds((b * tiles + t) * SUB, SUB), slice(v * LANES, (v + 1) * LANES)

            def find(b, carry):
                own, got = carry
                where = pos_ref[:, at : at + LANES] - (up + b * tiles * SUB)
                for t in range(tiles):
                    hit = where == t * SUB
                    own = own + jnp.where(hit, ids(b, t), 0.0)
                    got = got + jnp.where(hit, score_ref[place(b, t)], 0.0)
                return own, got

            own, got = repeat(blocks, find, (zero, zero))
            own = jnp.broadcast_to(jnp.sum(own, axis=0, keepdims=True), (SUB, LANES))
            got = jnp.sum(got, axis=0, keepdims=True)

            def mask(b, high):
                for t in range(tiles):
                    masked = jnp.where(ids(b, t) == own, LOW, score_ref[place(b, t)])
                    score_ref[place(b, t)] = masked
                    high = jnp.maximum(high, masked)
                return high

            high = repeat(blocks, mask, zero + LOW)
            top = jnp.maximum(jnp.max(high, axis=0, keepdims=True), got)
            high = jnp.broadcast_to(top, (SUB, LANES))

            def add(b, summed):
                for t in range(tiles):
                    summed = summed + jnp.exp2((score_ref[place(b, t)] - high) * rate)
                return summed

            summed = jnp.sum(repeat(blocks, add, zero), axis=0, keepdims=True)
            summed = summed + jnp.exp2((got - top) * rate)
            out_ref[:, at : at + LANES] = 0.125 * (top - got) + jnp.log(summed)


def losses(pool, users, positives, rows):
    devices = pool.shape[0]
    count, _ = users.shape
    wide = min(count, 2 * LANES)
    limit = (8 << 20) + 4 * devices * rows * wide + 4 * devices * rows * LANES + 2 * pool.nbytes
    return pl.pallas_call(
        functools.partial(loss_kernel, rows),
        out_shape=jax.ShapeDtypeStruct((1, count), jnp.float32),
        in_specs=[pl.BlockSpec(memory_space=pltpu.VMEM)] * 3,
        out_specs=pl.BlockSpec(memory_space=pltpu.VMEM),
        scratch_shapes=[
            pltpu.VMEM((devices * rows, wide), jnp.float32),
            pltpu.VMEM((devices * SUB, rows // SUB * LANES), jnp.float32),
        ],
        compiler_params=pltpu.CompilerParams(vmem_limit_bytes=limit),
        name="losses",
    )(pool, users, positives.reshape(1, count)).reshape(count)


def per_device(axes, devices, users, positives, items, item_ids):
    rows = items.shape[0]
    sent = pack(items, item_ids, devices)
    pool = lax.all_to_all(sent, axes, 0, 0, tiled=False)
    return losses(pool, users, positives, rows)


def solution(mesh):
    axes = ("row", "col")
    devices = mesh.shape["row"] * mesh.shape["col"]
    both = P(axes)
    return jax.shard_map(
        functools.partial(per_device, axes, devices),
        mesh=mesh,
        in_specs=(P(axes, None), both, P(axes, None), both),
        out_specs=both,
        check_vma=False,
    )
```

time: 123 us -> 23.1 us (0.19)
  blocking collectives: 109 us -> 19.2 us
  local copies, waits for them, and re-layouts: 11.3 us -> 1.36 us
  Pallas kernels: 0 us -> 2.36 us
  other arithmetic: 1.67 us -> 0 us
    all_gather x1 -> x0, blocking collectives: 67.4 us -> none  [per_device(): piece = lax.all_gather(items, ('row', 'col'), axis=0, tiled=True)]
    unnamed x1 -> x0, blocking collectives: 42 us -> none
    all_to_all x0 -> x1, blocking collectives: none -> 19.2 us  [per_device(): pool = lax.all_to_all(sent, axes, 0, 0, tiled=False)]
    gather x2 -> x0, local copies, waits for them, and re-layouts: 10.4 us -> none  [the longest x1 6.87 us: per_device(): pos_id = jnp.take(table, positives)]
    pallas_call x0 -> x2, Pallas kernels: none -> 2.36 us  [the longest x1 1.77 us: losses(): pl.pallas_call(functools.partial(loss_kernel, rows), out_shape=jax.ShapeD...]
where the time goes in v1:
time: 23.1 us; the launch traced here: 22.9 us
  blocking collectives  19.2 us (83%)
  Pallas kernels  2.36 us (10%)
  local copies, waits for them, and re-layouts  1.36 us (6%)
    all_to_all x1, blocking collectives, per_device(): pool = lax.all_to_all(sent, axes, 0, 0, tiled=False)  19.2 us
    pallas_call x1, Pallas kernels, losses(): pl.pallas_call(functools.partial(loss_kernel, rows), out_shape=jax.ShapeD...  1.77 us
    unnamed x8, local copies, waits for them, and re-layouts  1.36 us
    pallas_call x1, Pallas kernels, pack(): pl.pallas_call(pack_kernel, out_shape=jax.ShapeDtypeStruct((copies, tall,...  0.59 us

profile of v1, /device:TPU:0, one launch (start us, length us, event | category | flops | bytes accessed | tf_op | source)
XLA Modules:
  0.0 22.9 jit_solution(5708516096914926885)
XLA Ops:
  0.0 0.0 copy-start.1
  0.0 0.7 %copy-done.1 = bf16[16,256]{1,0:T(8,128)(2,1)S(1)} copy-done((bf16[16,256]{1,0:T(8,128)(2,1)S(1)}, bf16[16,256]{1,0:T(8,128)(2,1)}, u32[]{:S(2)}) %copy-start.1) | copy-done | bytes 8216
  0.7 0.0 copy-start.3
  0.7 0.7 %copy-done.3 = s32[16]{0:T(128)S(1)} copy-done((s32[16]{0:T(128)S(1)}, s32[16]{0:T(128)}, u32[]{:S(2)}) %copy-start.3) | copy-done | bytes 88
  1.4 0.0 copy-start
  1.4 0.6 %pack.1 = bf16[32,40,128]{2,1,0:T(8,128)(2,1)S(1)} custom-call(bf16[16,256]{1,0:T(8,128)(2,1)S(1)} %copy-done.1, s32[16]{0:T(128)S(1)} %copy-done.3), custom_call_target="tpu_custom_call" | custom-call | tf_op jit(solution)/shard_map/pack/pallas_call | solution.py:45
  2.0 0.0 copy-start.2
  2.0 19.2 %all_to_all.5.pool_ref = bf16[32,40,128]{2,1,0:T(8,128)(2,1)S(1)} all-to-all(bf16[32,40,128]{2,1,0:T(8,128)(2,1)S(1)} %pack.1), channel_id=1, replica_groups=mesh['row'=4,'col'=8] {'row','col'}, dimensions={0} | all-to-all | bytes 655360 | tf_op jit(solution)/shard_map/all_to_all | solution.py:176
  21.1 0.0 copy-done
  21.1 0.0 copy-done.2
  21.1 1.8 %losses.1 = f32[1,1024]{1,0:T(1,128)} custom-call(bf16[32,40,128]{2,1,0:T(8,128)(2,1)S(1)} %all_to_all.5.pool_ref, bf16[1024,256]{1,0:T(8,128)(2,1)S(1)} %copy-done, s32[1,1024]{1,0:T(1,128)S(1)} %bitcast.2), custom_call_target="tpu_custom_call" | custom-call | tf_op jit(solution)/shard_map/losses/pallas_call | solution.py:159
Async XLA Ops:
  0.0 0.7 %copy-start.1 = (bf16[16,256]{1,0:T(8,128)(2,1)S(1)}, bf16[16,256]{1,0:T(8,128)(2,1)}, u32[]{:S(2)}) copy-start(bf16[16,256]{1,0:T(8,128)(2,1)} %items_ref.1) | copy-start | bytes 24580
  0.7 0.7 %copy-start.3 = (s32[16]{0:T(128)S(1)}, s32[16]{0:T(128)}, u32[]{:S(2)}) copy-start(s32[16]{0:T(128)} %ids_ref.1) | copy-start | bytes 196
  1.4 19.8 %copy-start = (bf16[1024,256]{1,0:T(8,128)(2,1)S(1)}, bf16[1024,256]{1,0:T(8,128)(2,1)}, u32[]{:S(2)}) copy-start(bf16[1024,256]{1,0:T(8,128)(2,1)} %users_ref.1) | copy-start | bytes 1572868
  2.0 19.2 %copy-start.2 = (s32[1024]{0:T(1024)S(1)}, s32[1024]{0:T(1024)}, u32[]{:S(2)}) copy-start(s32[1024]{0:T(1024)} %param.5) | copy-start | bytes 12292

commit v2 on v1

v2 whole, which is shorter than its diff:
```python
import functools
import math
import random

import jax
import jax.numpy as jnp
from jax import lax
from jax.experimental import pallas as pl
from jax.experimental.pallas import tpu as pltpu
from jax.sharding import Mesh
from jax.sharding import PartitionSpec as P

LANES = 128
SUB = 8
BASE = 256
DIGITS = 3
LOW = -1e30
RATE = 0.125 / math.log(2)
SEED = 126


def pack_kernel(items_hbm, ids_hbm, out_ref, items_ref, ids_ref, sems):
    rows, width = items_ref.shape
    groups = rows // SUB
    span = LANES // groups
    copies = out_ref.shape[0]
    get_items = pltpu.make_async_copy(items_hbm, items_ref, sems.at[0])
    get_ids = pltpu.make_async_copy(ids_hbm, ids_ref, sems.at[1])
    get_ids.start()
    get_items.start()
    row = lax.broadcasted_iota(jnp.int32, (SUB, LANES), 0)
    lane = lax.broadcasted_iota(jnp.int32, (SUB, LANES), 1)
    get_ids.wait()
    held = jnp.zeros((SUB, LANES), jnp.int32)
    for k in range(rows):
        group = k // SUB
        mine = (row == k % SUB) & (lane >= group * span) & (lane < (group + 1) * span)
        held = jnp.where(mine, ids_ref[k], held)
    place = lane % span
    digit = jnp.zeros((SUB, LANES), jnp.int32)
    for d in range(DIGITS):
        digit = jnp.where(place == d, (held // BASE**d) % BASE, digit)
    tail = digit.astype(jnp.float32).astype(jnp.bfloat16)
    get_items.wait()
    cols = [items_ref[:, c * LANES : (c + 1) * LANES] for c in range(width // LANES)]
    for n in range(copies):
        for c, col in enumerate(cols):
            out_ref[n, c * rows : (c + 1) * rows, :] = col
        out_ref[n, len(cols) * rows :, :] = tail


def pack(items, ids, copies):
    rows, width = items.shape
    tall = rows * (width // LANES) + SUB
    return pl.pallas_call(
        pack_kernel,
        out_shape=jax.ShapeDtypeStruct((copies, tall, LANES), items.dtype),
        in_specs=[pl.BlockSpec(memory_space=pltpu.HBM)] * 2,
        out_specs=pl.BlockSpec(memory_space=pltpu.VMEM),
        scratch_shapes=[
            pltpu.VMEM((rows, width), items.dtype),
            pltpu.SMEM((rows,), jnp.int32),
            pltpu.SemaphoreType.DMA((2,)),
        ],
        compiler_params=pltpu.CompilerParams(vmem_limit_bytes=(2 << 20) + 4 * copies * tall * LANES),
        cost_estimate=pl.CostEstimate(flops=1 << 30, bytes_accessed=1 << 22, transcendentals=0),
        name="pack",
    )(pltpu.with_memory_space_constraint(items, pltpu.HBM), pltpu.with_memory_space_constraint(ids, pltpu.HBM))


def chunk_of(chips, rows):
    return math.gcd(chips, max(1, 256 // rows))


def weights(rows):
    groups = rows // SUB
    span = LANES // groups
    k = lax.broadcasted_iota(jnp.int32, (LANES, groups * LANES), 0)
    g = lax.broadcasted_iota(jnp.int32, (LANES, groups * LANES), 1) // LANES
    weigh = jnp.zeros((LANES, groups * LANES), jnp.float32)
    for d in range(DIGITS):
        weigh = jnp.where(k == g * span + d, float(BASE**d), weigh)
    return weigh.astype(jnp.bfloat16)


class Pool:
    def __init__(self, rows, order, columns, side, pool_ref, id_ref, score_ref):
        self.rows, self.order, self.columns = rows, order, columns
        self.pool, self.id, self.score = pool_ref, id_ref, score_ref
        self.offset = side * columns * rows
        self.chips, tall, _ = pool_ref.shape
        self.cols = (tall - SUB) // rows
        self.groups = rows // SUB
        self.batch = chunk_of(self.chips, rows)
        self.blocks = self.chips // self.batch
        self.tiles = self.batch * self.groups

    def repeat(self, body, init):
        return body(0, init) if self.blocks == 1 else lax.fori_loop(0, self.blocks, body, init)

    def decode(self):
        weigh = weights(self.rows)

        def body(b, _):
            digit = self.pool[pl.ds(b * self.batch, self.batch), self.cols * self.rows :, :]
            self.id[pl.ds(b * self.batch * SUB, self.batch * SUB), :] = jnp.dot(
                digit.reshape(self.batch * SUB, LANES), weigh, preferred_element_type=jnp.float32
            )
            return 0

        self.repeat(body, 0)

    def ids(self, b, t):
        d, g = divmod(t, self.groups)
        return self.id[pl.ds((b * self.batch + d) * SUB, SUB), g * LANES : (g + 1) * LANES]

    def first(self, b, t):
        d, g = divmod(t, self.groups)
        chip = self.order[d] if self.blocks == 1 else b * self.batch + d
        return ((chip // self.columns) * 2 * self.columns + chip % self.columns) * self.rows + g * SUB

    def place(self, b, t, lane):
        return pl.ds((b * self.tiles + t) * SUB, SUB), slice(lane, lane + LANES)

    def multiply(self, users, lane):
        def body(b, _):
            size = self.batch * self.rows
            left = jnp.concatenate(
                [
                    self.pool[pl.ds(b * self.batch, self.batch), c * self.rows : (c + 1) * self.rows, :]
                    .reshape(size, LANES)
                    for c in range(self.cols)
                ],
                axis=1,
            )
            self.score[pl.ds(b * size, size), lane : lane + users.shape[0]] = lax.dot_general(
                left, users, (((1,), (1,)), ((), ())), preferred_element_type=jnp.float32
            )
            return 0

        self.repeat(body, 0)

    def find(self, wanted, lane, carry):
        where = wanted - (lax.broadcasted_iota(jnp.int32, (SUB, LANES), 0) + self.offset)

        def body(b, carry):
            own, got = carry
            for t in range(self.tiles):
                hit = where == self.first(b, t)
                own = jnp.where(hit, self.ids(b, t), own)
                got = jnp.where(hit, self.score[self.place(b, t, lane)], got)
            return own, got

        return self.repeat(body, carry)

    def mask(self, own, lane, masked_ref, to, high):
        def body(b, high):
            for t in range(self.tiles):
                masked = jnp.where(self.ids(b, t) == own, LOW, self.score[self.place(b, t, lane)])
                masked_ref[self.place(b, t, to)] = masked
                high = jnp.maximum(high, masked)
            return high

        return self.repeat(body, high)

    def add(self, masked_ref, to, high, summed):
        def body(b, summed):
            for t in range(self.tiles):
                summed = summed + jnp.exp2((masked_ref[self.place(b, t, to)] - high) * RATE)
            return summed

        return self.repeat(body, summed)


def near_kernel(rows, order, columns, wide, pool_ref, users_ref, pos_ref, score_ref, id_ref, own_ref, got_ref):
    side = (lax.axis_index("d") // columns) % 2
    pool = Pool(rows, order, columns, side, pool_ref, id_ref, score_ref)
    pool.decode()
    zero = jnp.zeros((SUB, LANES), jnp.float32)
    for u in range(0, users_ref.shape[0], wide):
        pool.multiply(users_ref[u : u + wide, :], u)
        for at in range(u, u + wide, LANES):
            own, got = pool.find(pos_ref[:, at : at + LANES], at, (zero, zero))
            own_ref[:, at : at + LANES] = own
            got_ref[:, at : at + LANES] = got


def far_kernel(
    rows, order, columns, wide, pool_ref, users_ref, pos_ref, near_ref, near_id_ref, own_ref, got_ref,
    out_ref, score_ref, id_ref, masked_ref,
):
    side = (lax.axis_index("d") // columns) % 2
    near = Pool(rows, order, columns, side, pool_ref, near_id_ref, near_ref)
    far = Pool(rows, order, columns, 1 - side, pool_ref, id_ref, score_ref)
    far.decode()
    for u in range(0, users_ref.shape[0], wide):
        far.multiply(users_ref[u : u + wide, :], 0)
        for v in range(0, wide, LANES):
            at = u + v
            carry = own_ref[:, at : at + LANES], got_ref[:, at : at + LANES]
            own, got = far.find(pos_ref[:, at : at + LANES], v, carry)
            own = jnp.broadcast_to(jnp.sum(own, axis=0, keepdims=True), (SUB, LANES))
            got = jnp.sum(got, axis=0, keepdims=True)
            high = jnp.full((SUB, LANES), LOW, jnp.float32)
            high = near.mask(own, at, masked_ref, v, high)
            high = far.mask(own, v, score_ref, v, high)
            top = jnp.maximum(jnp.max(high, axis=0, keepdims=True), got)
            high = jnp.broadcast_to(top, (SUB, LANES))
            summed = jnp.zeros((SUB, LANES), jnp.float32)
            summed = near.add(masked_ref, v, high, summed)
            summed = far.add(score_ref, v, high, summed)
            summed = jnp.sum(summed, axis=0, keepdims=True) + jnp.exp2((got - top) * RATE)
            out_ref[:, at : at + LANES] = 0.125 * (top - got) + jnp.log(summed)


def sizes(pool, count, rows):
    chips = pool.shape[0]
    return chips * rows, min(count, 2 * LANES), (chips * SUB, rows // SUB * LANES)


def start_near(pool, users, positives, rows, order, columns):
    count, width = users.shape
    tall, wide, ids = sizes(pool, count, rows)
    limit = (6 << 20) + 4 * tall * count + 4 * math.prod(ids)
    vmem = pl.BlockSpec(memory_space=pltpu.VMEM)
    return pl.pallas_call(
        functools.partial(near_kernel, rows, order, columns, wide),
        out_shape=[
            jax.ShapeDtypeStruct((tall, count), jnp.float32),
            jax.ShapeDtypeStruct(ids, jnp.float32),
            jax.ShapeDtypeStruct((SUB, count), jnp.float32),
            jax.ShapeDtypeStruct((SUB, count), jnp.float32),
        ],
        in_specs=[vmem] * 3,
        out_specs=[vmem] * 4,
        compiler_params=pltpu.CompilerParams(vmem_limit_bytes=limit + 2 * pool.nbytes),
        cost_estimate=pl.CostEstimate(
            flops=2 * tall * count * width, bytes_accessed=users.nbytes, transcendentals=0
        ),
        name="near",
    )(pool, users, positives)


def finish_far(pool, users, positives, held, rows, order, columns):
    count, width = users.shape
    tall, wide, ids = sizes(pool, count, rows)
    limit = (6 << 20) + 4 * tall * (count + 2 * wide) + 8 * math.prod(ids)
    vmem = pl.BlockSpec(memory_space=pltpu.VMEM)
    return pl.pallas_call(
        functools.partial(far_kernel, rows, order, columns, wide),
        out_shape=jax.ShapeDtypeStruct((1, count), jnp.float32),
        in_specs=[vmem] * 7,
        out_specs=vmem,
        scratch_shapes=[
            pltpu.VMEM((tall, wide), jnp.float32),
            pltpu.VMEM(ids, jnp.float32),
            pltpu.VMEM((tall, wide), jnp.float32),
        ],
        compiler_params=pltpu.CompilerParams(vmem_limit_bytes=limit + 2 * pool.nbytes),
        name="far",
    )(pool, users, positives, *held).reshape(count)


def per_device(columns, chips, users, positives, items, item_ids):
    rows = items.shape[0]
    order = list(range(chips))
    if chunk_of(chips, rows) == chips:
        random.Random(SEED).shuffle(order)

    def device(chip, side):
        return (chip // columns * 2 + side) * columns + chip % columns

    groups = [[device(chip, side) for chip in order] for side in range(2)]
    swaps = [(device(chip, side), device(chip, 1 - side)) for chip in order for side in range(2)]
    sent = pack(items, item_ids, chips)
    near = lax.all_to_all(sent, "d", 0, 0, tiled=False, axis_index_groups=groups)
    far = lax.ppermute(near, "d", swaps)
    wanted = positives.reshape(1, -1)
    held = start_near(near, users, wanted, rows, order, columns)
    return finish_far(far, users, wanted, held, rows, order, columns)


def solution(mesh):
    columns = mesh.shape["col"]
    chips = mesh.shape["row"] // 2 * columns
    flat = Mesh(mesh.devices.reshape(-1), ("d",))
    return jax.shard_map(
        functools.partial(per_device, columns, chips),
        mesh=flat,
        in_specs=(P("d", None), P("d"), P("d", None), P("d")),
        out_specs=P("d"),
        check_vma=False,
    )
```

time: 23.1 us -> 16.9 us (0.73)
  blocking collectives: 19.2 us -> 12.9 us
  local copies, waits for them, and re-layouts: 1.36 us -> 0.01 us
  waiting for transfers between devices: 0 us -> 0.99 us
  Pallas kernels: 2.36 us -> 2.75 us
    all_to_all x1, blocking collectives: 19.2 us -> 12.9 us  [per_device(): lax.all_to_all(sent, 'd', 0, 0, tiled=False, axis_index_groups=groups)]
    unnamed x8 -> x4, local copies, waits for them, and re-layouts: 1.36 us -> 0.01 us
    ppermute x0 -> x1, waiting for transfers between devices: none -> 0.99 us  [per_device(): far = lax.ppermute(near, 'd', swaps)]
    pallas_call x1, Pallas kernels: 0.59 us -> 0.87 us  [pack(): pl.pallas_call(pack_kernel, out_shape=jax.ShapeDtypeStruct((copies, tall,...]
    pallas_call x1 -> x2, Pallas kernels: 1.77 us -> 1.88 us  [the longest x1 1.5 us: finish_far(): pl.pallas_call(functools.partial(far_kernel, rows, order, columns, wide),...]
  transfers between devices with their start and end apart: 0 -> 1, of which waited for: 0 -> 1; matrix products, arithmetic and copies ran while one was open for 0% -> 0% of each run, Pallas kernels for 0% -> 2%
where the time goes in v2:
time: 16.9 us; the launch traced here: 16.7 us
  blocking collectives  12.9 us (76%)
  Pallas kernels  2.75 us (16%)
  waiting for transfers between devices  0.99 us (6%)
    all_to_all x1, blocking collectives, per_device(): lax.all_to_all(sent, 'd', 0, 0, tiled=False, axis_index_groups=groups)  12.9 us
    pallas_call x1, Pallas kernels, finish_far(): pl.pallas_call(functools.partial(far_kernel, rows, order, columns, wide),...  1.5 us
    ppermute x1, waiting for transfers between devices, per_device(): far = lax.ppermute(near, 'd', swaps)  0.99 us
    pallas_call x1, Pallas kernels, pack(): pl.pallas_call(pack_kernel, out_shape=jax.ShapeDtypeStruct((copies, tall,...  0.87 us
    pallas_call x1, Pallas kernels, start_near(): pl.pallas_call(functools.partial(near_kernel, rows, order, columns, wide)...  0.39 us
  transfers between devices with their start and end apart: 1, of which 1 were waited for; matrix products, arithmetic and copies ran while one was open for 0% of the time, Pallas kernels for 2%

profile of v2, /device:TPU:0, one launch (start us, length us, event | category | flops | bytes accessed | tf_op | source)
XLA Modules:
  0.0 16.7 jit_solution(14036301484633972470)
XLA Ops:
  0.0 0.0 copy-start
  0.0 0.9 %pack.1 = bf16[16,40,128]{2,1,0:T(8,128)(2,1)S(1)} custom-call(bf16[16,256]{1,0:T(8,128)(2,1)} %items_hbm.1, s32[16]{0:T(128)} %ids_hbm.1), custom_call_target="tpu_custom_call" | custom-call | flops 1073741824 | bytes 4194304 | tf_op jit(solution)/shard_map/pack/pallas_call | solution.py:55
  0.9 0.0 copy-start.1
  0.9 12.9 %all_to_all.5.pool_ref = bf16[16,40,128]{2,1,0:T(8,128)(2,1)S(1)} all-to-all(bf16[16,40,128]{2,1,0:T(8,128)(2,1)S(1)} %pack.1), channel_id=1, replica_groups={{21,4,0,19,5,6,23,16,20,2,18,3,7,22,17,1},{29,12,8,27,13,14,31,24,28,10..., dimensions={0} | all-to-all | bytes 327680 | tf_op jit(solution)/shard_map/all_to_all | solution.py:276
  13.8 0.0 collective-permute-start
  13.8 0.0 copy-done
  13.8 0.0 copy-done.1
  13.8 0.4 %near.1 = (f32[256,1024]{1,0:T(8,128)S(1)}, f32[128,256]{1,0:T(8,128)S(1)}, f32[8,1024]{1,0:T(8,128)S(1)}, f32[8,1024]{1,0:T(8,128)S(1)}) custom-call(bf16[16,40,128]{2,1,0:T(8,128)(2,1)S(1)} %all_to_all.5.pool_ref, bf16[1024,256]{1,0:T(8,128)(2,1)S(1)} %copy-done, s32[1,1024]{1,0:T(1,128)S(1)} %bitcast.2), custom_call_target="tpu_custom_call" | custom-call | flops 134217728 | bytes 524288 | tf_op jit(solution)/shard_map/near/pallas_call | solution.py:226
  14.2 1.0 %collective-permute-done.pool_ref = bf16[16,40,128]{2,1,0:T(8,128)(2,1)S(1)} collective-permute-done((bf16[16,40,128]{2,1,0:T(8,128)(2,1)S(1)}, bf16[16,40,128]{2,1,0:T(8,128)(2,1)S(1)}, u32[]{:S(2)}, u32[]{:S(2)}) %collective-permute-start) | collective-permute-done | bytes 163872 | tf_op jit(solution)/shard_map/ppermute | solution.py:277
  15.2 1.5 %far.1 = f32[1,1024]{1,0:T(1,128)} custom-call(bf16[16,40,128]{2,1,0:T(8,128)(2,1)S(1)} %collective-permute-done.pool_ref, bf16[1024,256]{1,0:T(8,128)(2,1)S(1)} %copy-done, s32[1,1024]{1,0:T(1,128)S(1)} %bitcast.3, f32[256,1024]{1,0:T(8,128)S(1)} %get-tuple-element.9.near_ref, f32[128,256]{1,0:T(8,128)S(1)} %get-tuple-element.10.near_id_ref, ...), custom_call_target="tpu_custom_call" | custom-call | tf_op jit(solution)/shard_map/far/pallas_call | solution.py:249
Async XLA Ops:
  0.0 13.8 %copy-start = (bf16[1024,256]{1,0:T(8,128)(2,1)S(1)}, bf16[1024,256]{1,0:T(8,128)(2,1)}, u32[]{:S(2)}) copy-start(bf16[1024,256]{1,0:T(8,128)(2,1)} %users_ref.3) | copy-start | bytes 1572868
  0.9 12.9 %copy-start.1 = (s32[1024]{0:T(1024)S(1)}, s32[1024]{0:T(1024)}, u32[]{:S(2)}) copy-start(s32[1024]{0:T(1024)} %param.5) | copy-start | bytes 12292
  13.8 1.4 %collective-permute-start = (bf16[16,40,128]{2,1,0:T(8,128)(2,1)S(1)}, bf16[16,40,128]{2,1,0:T(8,128)(2,1)S(1)}, u32[]{:S(2)}, u32[]{:S(2)}) collective-permute-start(bf16[16,40,128]{2,1,0:T(8,128)(2,1)S(1)} %all_to_all.5.pool_ref), channel_id=1, source_target_pairs={{21,29},{29,21},{4,12},{12,4},{0,8},{8,0},{19,27},{27,19},{5,13},{... | collective-permute-start | bytes 491528 | tf_op jit(solution)/shard_map/ppermute | solution.py:277

commit v3 on v2

--- a/solution.py
+++ b/solution.py
@@ -1,6 +1,5 @@
 import functools
 import math
-import random
 
 import jax
 import jax.numpy as jnp
@@ -16,7 +15,9 @@
 DIGITS = 3
 LOW = -1e30
 RATE = 0.125 / math.log(2)
-SEED = 126
+REACH = 40.0
+ORDER = (13, 4, 0, 11, 1, 5, 8, 10, 12, 2, 3, 6, 7, 14, 9, 15)
+TURNED = (0, 3, 10)
 
 
 def pack_kernel(items_hbm, ids_hbm, out_ref, items_ref, ids_ref, sems):
@@ -84,10 +85,11 @@
 
 
 class Pool:
-    def __init__(self, rows, order, columns, side, pool_ref, id_ref, score_ref):
-        self.rows, self.order, self.columns = rows, order, columns
+    def __init__(self, rows, plan, columns, group, pool_ref, id_ref, score_ref):
+        self.rows, self.columns = rows, columns
+        self.order, self.turned = plan
         self.pool, self.id, self.score = pool_ref, id_ref, score_ref
-        self.offset = side * columns * rows
+        self.group = group
         self.chips, tall, _ = pool_ref.shape
         self.cols = (tall - SUB) // rows
         self.groups = rows // SUB
@@ -114,13 +116,14 @@
         d, g = divmod(t, self.groups)
         return self.id[pl.ds((b * self.batch + d) * SUB, SUB), g * LANES : (g + 1) * LANES]
 
-    def first(self, b, t):
-        d, g = divmod(t, self.groups)
-        chip = self.order[d] if self.blocks == 1 else b * self.batch + d
+    def chip(self, b, d):
+        return self.order[d] if self.blocks == 1 else b * self.batch + d
+
+    def first(self, chip, g):
         return ((chip // self.columns) * 2 * self.columns + chip % self.columns) * self.rows + g * SUB
 
     def place(self, b, t, lane):
-        return pl.ds((b * self.tiles + t) * SUB, SUB), slice(lane, lane + LANES)
+        return pl.ds((b * self.tiles + t) * SUB, SUB), pl.ds(lane, LANES)
 
     def multiply(self, users, lane):
         def body(b, _):
@@ -141,76 +144,166 @@
         self.repeat(body, 0)
 
     def find(self, wanted, lane, carry):
-        where = wanted - (lax.broadcasted_iota(jnp.int32, (SUB, LANES), 0) + self.offset)
+        up = lax.broadcasted_iota(jnp.int32, (SUB, LANES), 0)
+        step = self.columns * self.rows
+        straight = wanted - (up + self.group * step)
+        crossed = wanted - (up + (1 - self.group) * step) if self.turned else straight
 
         def body(b, carry):
-            own, got = carry
-            for t in range(self.tiles):
-                hit = where == self.first(b, t)
+            own, got, peak = carry
+            for t in range(self.tiles):
+                chip = self.chip(b, t // self.groups)
+                where = crossed if self.turned and chip in self.turned else straight
+                hit = where == self.first(chip, t % self.groups)
+                score = self.score[self.place(b, t, lane)]
                 own = jnp.where(hit, self.ids(b, t), own)
-                got = jnp.where(hit, self.score[self.place(b, t, lane)], got)
-            return own, got
+                got = jnp.where(hit, score, got)
+                peak = jnp.maximum(peak, score)
+            return own, got, peak
 
         return self.repeat(body, carry)
 
-    def mask(self, own, lane, masked_ref, to, high):
+    def raise_to(self, lane, high, term_ref):
+        def body(b, _):
+            for t in range(self.tiles):
+                at = self.place(b, t, lane)
+                term_ref[at] = jnp.exp2((self.score[at] - high) * RATE)
+            return 0
+
+        self.repeat(body, 0)
+
+    def add_raised(self, own, lane, term_ref, summed):
+        def body(b, summed):
+            for t in range(self.tiles):
+                summed = summed + jnp.where(self.ids(b, t) == own, 0.0, term_ref[self.place(b, t, lane)])
+            return summed
+
+        return self.repeat(body, summed)
+
+    def kept(self, own, b, t, lane):
+        return jnp.where(self.ids(b, t) == own, LOW, self.score[self.place(b, t, lane)])
+
+    def add(self, own, lane, high, summed):
+        def body(b, summed):
+            for t in range(self.tiles):
+                summed = summed + jnp.exp2((self.kept(own, b, t, lane) - high) * RATE)
+            return summed
+
+        return self.repeat(body, summed)
+
+    def highest(self, own, lane, high):
         def body(b, high):
             for t in range(self.tiles):
-                masked = jnp.where(self.ids(b, t) == own, LOW, self.score[self.place(b, t, lane)])
-                masked_ref[self.place(b, t, to)] = masked
-                high = jnp.maximum(high, masked)
+                high = jnp.maximum(high, self.kept(own, b, t, lane))
             return high
 
         return self.repeat(body, high)
 
-    def add(self, masked_ref, to, high, summed):
-        def body(b, summed):
-            for t in range(self.tiles):
-                summed = summed + jnp.exp2((masked_ref[self.place(b, t, to)] - high) * RATE)
-            return summed
-
-        return self.repeat(body, summed)
-
-
-def near_kernel(rows, order, columns, wide, pool_ref, users_ref, pos_ref, score_ref, id_ref, own_ref, got_ref):
-    side = (lax.axis_index("d") // columns) % 2
-    pool = Pool(rows, order, columns, side, pool_ref, id_ref, score_ref)
+
+def spread(row):
+    return jnp.broadcast_to(row, (SUB, LANES))
+
+
+def total(x):
+    return jnp.sum(x, axis=0, keepdims=True)
+
+
+def group_of(columns, turned):
+    row, column = lax.axis_index("d") // columns, lax.axis_index("d") % columns
+    chip = row // 2 * columns + column
+    flips = sum(1 << k for k in turned)
+    return row % 2 if not turned else (row + (lax.shift_right_logical(jnp.int32(flips), chip) & 1)) % 2
+
+
+def near_kernel(
+    rows, plan, columns, wide, pool_ref, users_ref, pos_ref,
+    score_ref, id_ref, own_ref, got_ref, top_ref, *term_ref,
+):
+    group = group_of(columns, plan[1])
+    pool = Pool(rows, plan, columns, group, pool_ref, id_ref, score_ref)
     pool.decode()
     zero = jnp.zeros((SUB, LANES), jnp.float32)
     for u in range(0, users_ref.shape[0], wide):
         pool.multiply(users_ref[u : u + wide, :], u)
         for at in range(u, u + wide, LANES):
-            own, got = pool.find(pos_ref[:, at : at + LANES], at, (zero, zero))
-            own_ref[:, at : at + LANES] = own
-            got_ref[:, at : at + LANES] = got
+            here = pl.ds(at, LANES)
+            own, got, peak = pool.find(pos_ref[:, here], at, (zero, zero, zero + LOW))
+            own_ref[:, here] = own
+            got_ref[:, here] = got
+            top = jnp.max(peak, axis=0, keepdims=True)
+            top_ref[:, here] = top
+            if term_ref:
+                pool.raise_to(at, spread(top), term_ref[0])
 
 
 def far_kernel(
-    rows, order, columns, wide, pool_ref, users_ref, pos_ref, near_ref, near_id_ref, own_ref, got_ref,
-    out_ref, score_ref, id_ref, masked_ref,
+    rows, plan, columns, wide, pool_ref, users_ref, pos_ref, near_ref, near_id_ref, own_ref, got_ref, top_ref,
+    *refs,
 ):
-    side = (lax.axis_index("d") // columns) % 2
-    near = Pool(rows, order, columns, side, pool_ref, near_id_ref, near_ref)
-    far = Pool(rows, order, columns, 1 - side, pool_ref, id_ref, score_ref)
+    term_ref = refs[:-5]
+    out_hbm, out_ref, score_ref, id_ref, sem = refs[-5:]
+    group = group_of(columns, plan[1])
+    near = Pool(rows, plan, columns, group, pool_ref, near_id_ref, near_ref)
+    far = Pool(rows, plan, columns, 1 - group, pool_ref, id_ref, score_ref)
+    zero = jnp.zeros((SUB, LANES), jnp.float32)
+
+    def settle(lane, got, top, summed):
+        summed = total(summed) + jnp.exp2((got - top) * RATE)
+        out_ref[:, pl.ds(lane, LANES)] = 0.125 * (top - got) + jnp.log(summed)
+
+    def find(lane, base):
+        here = pl.ds(lane, LANES)
+        carry = own_ref[:, here], got_ref[:, here], zero + LOW
+        own, got, peak = far.find(pos_ref[:, here], base, carry)
+        return spread(total(own)), total(got), jnp.max(peak, axis=0, keepdims=True)
+
+    def careful(lane, base, own, got):
+        high = far.highest(own, base, near.highest(own, lane, zero + LOW))
+        top = jnp.maximum(jnp.max(high, axis=0, keepdims=True), got)
+        summed = near.add(own, lane, spread(top), zero)
+        summed = far.add(own, base, spread(top), summed)
+        settle(lane, got, top, summed)
+
     far.decode()
+    worst = jnp.zeros((1, LANES), jnp.float32)
     for u in range(0, users_ref.shape[0], wide):
-        far.multiply(users_ref[u : u + wide, :], 0)
+        start = u if term_ref else 0
+        far.multiply(users_ref[u : u + wide, :], start)
         for v in range(0, wide, LANES):
-            at = u + v
-            carry = own_ref[:, at : at + LANES], got_ref[:, at : at + LANES]
-            own, got = far.find(pos_ref[:, at : at + LANES], v, carry)
-            own = jnp.broadcast_to(jnp.sum(own, axis=0, keepdims=True), (SUB, LANES))
-            got = jnp.sum(got, axis=0, keepdims=True)
-            high = jnp.full((SUB, LANES), LOW, jnp.float32)
-            high = near.mask(own, at, masked_ref, v, high)
-            high = far.mask(own, v, score_ref, v, high)
-            top = jnp.maximum(jnp.max(high, axis=0, keepdims=True), got)
-            high = jnp.broadcast_to(top, (SUB, LANES))
-            summed = jnp.zeros((SUB, LANES), jnp.float32)
-            summed = near.add(masked_ref, v, high, summed)
-            summed = far.add(score_ref, v, high, summed)
-            summed = jnp.sum(summed, axis=0, keepdims=True) + jnp.exp2((got - top) * RATE)
-            out_ref[:, at : at + LANES] = 0.125 * (top - got) + jnp.log(summed)
+            lane, base = u + v, start + v
+            own, got, peak = find(lane, base)
+            if not term_ref:
+                careful(lane, base, own, got)
+                continue
+            near_top = top_ref[:, pl.ds(lane, LANES)]
+            top = jnp.maximum(peak, near_top)
+            worst = jnp.maximum(worst, top - got)
+            summed = near.add_raised(own, lane, term_ref[0], zero)
+            summed = summed * spread(jnp.exp2((near_top - top) * RATE))
+            summed = far.add(own, base, spread(top), summed)
+            settle(lane, got, top, summed)
+
+    copy = pltpu.make_async_copy(out_ref, out_hbm, sem)
+    copy.start()
+    if term_ref:
+
+        @pl.when(jnp.max(worst) * RATE > REACH)
+        def _():
+            copy.wait()
+
+            @pl.loop(0, out_ref.shape[1] // LANES)
+            def _(n):
+                lane = pl.multiple_of(n * LANES, LANES)
+                own, got, _ = find(lane, lane)
+                careful(lane, lane, own, got)
+
+            copy.start()
+
+    copy.wait()
+
+
+def one_block(pool, rows):
+    return chunk_of(pool.shape[0], rows) == pool.shape[0]
 
 
 def sizes(pool, count, rows):
@@ -218,21 +311,24 @@
     return chips * rows, min(count, 2 * LANES), (chips * SUB, rows // SUB * LANES)
 
 
-def start_near(pool, users, positives, rows, order, columns):
+def start_near(pool, users, positives, rows, plan, columns):
     count, width = users.shape
     tall, wide, ids = sizes(pool, count, rows)
-    limit = (6 << 20) + 4 * tall * count + 4 * math.prod(ids)
+    raised = [jax.ShapeDtypeStruct((tall, count), jnp.float32)] if one_block(pool, rows) else []
+    limit = (6 << 20) + 4 * tall * count * (1 + len(raised)) + 4 * math.prod(ids)
     vmem = pl.BlockSpec(memory_space=pltpu.VMEM)
     return pl.pallas_call(
-        functools.partial(near_kernel, rows, order, columns, wide),
+        functools.partial(near_kernel, rows, plan, columns, wide),
         out_shape=[
             jax.ShapeDtypeStruct((tall, count), jnp.float32),
             jax.ShapeDtypeStruct(ids, jnp.float32),
             jax.ShapeDtypeStruct((SUB, count), jnp.float32),
             jax.ShapeDtypeStruct((SUB, count), jnp.float32),
+            jax.ShapeDtypeStruct((1, count), jnp.float32),
+            *raised,
         ],
         in_specs=[vmem] * 3,
-        out_specs=[vmem] * 4,
+        out_specs=[vmem] * (5 + len(raised)),
         compiler_params=pltpu.CompilerParams(vmem_limit_bytes=limit + 2 * pool.nbytes),
         cost_estimate=pl.CostEstimate(
             flops=2 * tall * count * width, bytes_accessed=users.nbytes, transcendentals=0
@@ -241,20 +337,22 @@
     )(pool, users, positives)
 
 
-def finish_far(pool, users, positives, held, rows, order, columns):
+def finish_far(pool, users, positives, held, rows, plan, columns):
     count, width = users.shape
     tall, wide, ids = sizes(pool, count, rows)
-    limit = (6 << 20) + 4 * tall * (count + 2 * wide) + 8 * math.prod(ids)
+    across = count if one_block(pool, rows) else wide
+    limit = (6 << 20) + 4 * tall * ((len(held) - 4) * count + across) + 8 * math.prod(ids)
     vmem = pl.BlockSpec(memory_space=pltpu.VMEM)
     return pl.pallas_call(
-        functools.partial(far_kernel, rows, order, columns, wide),
+        functools.partial(far_kernel, rows, plan, columns, wide),
         out_shape=jax.ShapeDtypeStruct((1, count), jnp.float32),
-        in_specs=[vmem] * 7,
-        out_specs=vmem,
+        in_specs=[vmem] * (3 + len(held)),
+        out_specs=pl.BlockSpec(memory_space=pltpu.HBM),
         scratch_shapes=[
-            pltpu.VMEM((tall, wide), jnp.float32),
+            pltpu.VMEM((1, count), jnp.float32),
+            pltpu.VMEM((tall, across), jnp.float32),
             pltpu.VMEM(ids, jnp.float32),
-            pltpu.VMEM((tall, wide), jnp.float32),
+            pltpu.SemaphoreType.DMA,
         ],
         compiler_params=pltpu.CompilerParams(vmem_limit_bytes=limit + 2 * pool.nbytes),
         name="far",
@@ -263,12 +361,15 @@
 
 def per_device(columns, chips, users, positives, items, item_ids):
     rows = items.shape[0]
-    order = list(range(chips))
+    order, turned = list(range(chips)), ()
     if chunk_of(chips, rows) == chips:
-        random.Random(SEED).shuffle(order)
+        size = len(ORDER)
+        order.sort(key=lambda chip: (ORDER.index(chip % size), chip))
+        turned = tuple(chip for chip in order if chip % size in TURNED)
+    plan = tuple(order), turned
 
     def device(chip, side):
-        return (chip // columns * 2 + side) * columns + chip % columns
+        return (chip // columns * 2 + (side ^ (chip in turned))) * columns + chip % columns
 
     groups = [[device(chip, side) for chip in order] for side in range(2)]
     swaps = [(device(chip, side), device(chip, 1 - side)) for chip in order for side in range(2)]
@@ -276,8 +377,8 @@
     near = lax.all_to_all(sent, "d", 0, 0, tiled=False, axis_index_groups=groups)
     far = lax.ppermute(near, "d", swaps)
     wanted = positives.reshape(1, -1)
-    held = start_near(near, users, wanted, rows, order, columns)
-    return finish_far(far, users, wanted, held, rows, order, columns)
+    held = start_near(near, users, wanted, rows, plan, columns)
+    return finish_far(far, users, wanted, held, rows, plan, columns)
 
 
 def solution(mesh):

time: 16.9 us -> 18.4 us (1.089)
  Pallas kernels: 2.75 us -> 5.01 us
  blocking collectives: 12.9 us -> 11.5 us
  starting transfers between devices: 0.01 us -> 1.11 us
  waiting for transfers between devices: 0.99 us -> 0.52 us
    pallas_call x2, Pallas kernels: 1.88 us -> 4.14 us  [the longest x1 3.64 us: finish_far(): pl.pallas_call(functools.partial(far_kernel, rows, plan, columns, wide),...]
    all_to_all x1, blocking collectives: 12.9 us -> 11.5 us  [per_device(): lax.all_to_all(sent, 'd', 0, 0, tiled=False, axis_index_groups=groups)]
    ppermute x1, starting transfers between devices: 0.01 us -> 1.11 us  [per_device(): far = lax.ppermute(near, 'd', swaps)]
    ppermute x1, waiting for transfers between devices: 0.99 us -> 0.52 us  [per_device(): far = lax.ppermute(near, 'd', swaps)]
  transfers between devices with their start and end apart: 1 -> 1, of which waited for: 1 -> 1; matrix products, arithmetic and copies ran while one was open for 0% -> 0% of each run, Pallas kernels for 2% -> 3%
where the time goes in v3:
time: 18.4 us; the launch traced here: 18.2 us
  blocking collectives  11.5 us (63%)
  Pallas kernels  5.01 us (27%)
  starting transfers between devices  1.11 us (6%)
  waiting for transfers between devices  0.52 us (3%)
    all_to_all x1, blocking collectives, per_device(): lax.all_to_all(sent, 'd', 0, 0, tiled=False, axis_index_groups=groups)  11.5 us
    pallas_call x1, Pallas kernels, finish_far(): pl.pallas_call(functools.partial(far_kernel, rows, plan, columns, wide),...  3.64 us
    ppermute x1, starting transfers between devices, per_device(): far = lax.ppermute(near, 'd', swaps)  1.11 us
    pallas_call x1, Pallas kernels, pack(): pl.pallas_call(pack_kernel, out_shape=jax.ShapeDtypeStruct((copies, tall,...  0.87 us
    ppermute x1, waiting for transfers between devices, per_device(): far = lax.ppermute(near, 'd', swaps)  0.52 us
    pallas_call x1, Pallas kernels, start_near(): pl.pallas_call(functools.partial(near_kernel, rows, plan, columns, wide),...  0.5 us
  transfers between devices with their start and end apart: 1, of which 1 were waited for; matrix products, arithmetic and copies ran while one was open for 0% of the time, Pallas kernels for 3%

profile of v3, /device:TPU:0, one launch (start us, length us, event | category | flops | bytes accessed | tf_op | source)
XLA Modules:
  0.0 18.2 jit_solution(8249066517011637499)
XLA Ops:
  0.0 0.0 copy-start
  0.0 0.9 %pack.1 = bf16[16,40,128]{2,1,0:T(8,128)(2,1)S(1)} custom-call(bf16[16,256]{1,0:T(8,128)(2,1)} %items_hbm.1, s32[16]{0:T(128)} %ids_hbm.1), custom_call_target="tpu_custom_call" | custom-call | flops 1073741824 | bytes 4194304 | tf_op jit(solution)/shard_map/pack/pallas_call | solution.py:56
  0.9 0.0 copy-start.1
  0.9 11.5 %all_to_all.5.pool_ref = bf16[16,40,128]{2,1,0:T(8,128)(2,1)S(1)} all-to-all(bf16[16,40,128]{2,1,0:T(8,128)(2,1)S(1)} %pack.1), channel_id=1, replica_groups={{21,4,8,19,1,5,16,26,20,2,11,6,7,22,17,23},{29,12,0,27,9,13,24,18,28,10..., dimensions={0} | all-to-all | bytes 327680 | tf_op jit(solution)/shard_map/all_to_all | solution.py:377
  12.4 1.1 %collective-permute-start = (bf16[16,40,128]{2,1,0:T(8,128)(2,1)S(1)}, bf16[16,40,128]{2,1,0:T(8,128)(2,1)S(1)}, u32[]{:S(2)}, u32[]{:S(2)}) collective-permute-start(bf16[16,40,128]{2,1,0:T(8,128)(2,1)S(1)} %all_to_all.5.pool_ref), channel_id=1, source_target_pairs={{21,29},{29,21},{4,12},{12,4},{8,0},{0,8},{19,27},{27,19},{1,9},{9... | collective-permute-start | bytes 491528 | tf_op jit(solution)/shard_map/ppermute | solution.py:378
  13.5 0.0 copy-done
  13.5 0.0 copy-done.1
  13.5 0.5 %near.1 = (f32[256,1024]{1,0:T(8,128)S(1)}, f32[128,256]{1,0:T(8,128)S(1)}, f32[8,1024]{1,0:T(8,128)S(1)}, f32[8,1024]{1,0:T(8,128)S(1)}, f32[1,1024]{1,0:T(1,128)S(1)}, /*index=5*/f32[256,1024]{1,0:T(8,128)S(1)}) custom-call(bf16[16,40,128]{2,1,0:T(8,128)(2,1)S(1)} %all_to_all.5.pool_ref, bf16[1024,256]{1,0:T(8,128)(2,1)S(1)} %copy-done, s32[1,1024]{1,0:T(1,128)S(1)} %bitcast.2), custom_call_target="tpu_custom_call" | custom-call | flops 134217728 | bytes 524288 | tf_op jit(solution)/shard_map/near/pallas_call | solution.py:320
  14.0 0.5 %collective-permute-done.pool_ref = bf16[16,40,128]{2,1,0:T(8,128)(2,1)S(1)} collective-permute-done((bf16[16,40,128]{2,1,0:T(8,128)(2,1)S(1)}, bf16[16,40,128]{2,1,0:T(8,128)(2,1)S(1)}, u32[]{:S(2)}, u32[]{:S(2)}) %collective-permute-start) | collective-permute-done | bytes 163872 | tf_op jit(solution)/shard_map/ppermute | solution.py:378
  14.5 3.6 %far.1 = f32[1,1024]{1,0:T(1,128)} custom-call(bf16[16,40,128]{2,1,0:T(8,128)(2,1)S(1)} %collective-permute-done.pool_ref, bf16[1024,256]{1,0:T(8,128)(2,1)S(1)} %copy-done, s32[1,1024]{1,0:T(1,128)S(1)} %bitcast.3, f32[256,1024]{1,0:T(8,128)S(1)} %get-tuple-element.11.near_ref, f32[128,256]{1,0:T(8,128)S(1)} %get-tuple-element.12.near_id_ref, ...), custom_call_target="tpu_custom_call" | custom-call | tf_op jit(solution)/shard_map/far/pallas_call | solution.py:346
Async XLA Ops:
  0.0 13.5 %copy-start = (bf16[1024,256]{1,0:T(8,128)(2,1)S(1)}, bf16[1024,256]{1,0:T(8,128)(2,1)}, u32[]{:S(2)}) copy-start(bf16[1024,256]{1,0:T(8,128)(2,1)} %users_ref.3) | copy-start | bytes 1572868
  0.9 12.6 %copy-start.1 = (s32[1024]{0:T(1024)S(1)}, s32[1024]{0:T(1024)}, u32[]{:S(2)}) copy-start(s32[1024]{0:T(1024)} %param.5) | copy-start | bytes 12292
  12.4 2.1 %collective-permute-start = (bf16[16,40,128]{2,1,0:T(8,128)(2,1)S(1)}, bf16[16,40,128]{2,1,0:T(8,128)(2,1)S(1)}, u32[]{:S(2)}, u32[]{:S(2)}) collective-permute-start(bf16[16,40,128]{2,1,0:T(8,128)(2,1)S(1)} %all_to_all.5.pool_ref), channel_id=1, source_target_pairs={{21,29},{29,21},{4,12},{12,4},{8,0},{0,8},{19,27},{27,19},{1,9},{9... | collective-permute-start | bytes 491528 | tf_op jit(solution)/shard_map/ppermute | solution.py:378
